TPU v7x, 32 devices: a whole 2x2x4 slice. The times are simulated.
32 devices in a mesh: row: 8 (over z, y), col: 4 (over x, core).
Axes of the slice: x: 2, y: 2, z: 4, core: 2. Of those that a mesh axis runs over, the one named last changes fastest.
Arguments:
- right_side: float32 [3, 64, 512], P(None, 'row', 'col'), may hold values from -6 to 6
- viscosity: float32 [64, 512], P('row', 'col'), may hold values from 0.1 to 3
- free_mask: int32 [3, 64, 512], P(None, 'row', 'col'), may hold values 0 or 1
- coarse_basis: float32 [64, 3, 64, 512], P(None, None, 'row', 'col'), may hold values from -6 to 6
- gram_inverse: float32 [64, 64], P('col'), may hold values from -3 to 6, as said below
Outputs:
- solution: float32 [3, 64, 512], P(None, 'row', 'col')
- residual: float32 [3, 64, 512], P(None, 'row', 'col')
Inputs may be any that keep to these rules, and one draw needn't show every extreme that they name: `free_mask`: 1 marks a free velocity unknown, 0 one whose value is prescribed. `gram_inverse`: symmetric positive definite.
All inputs are finite; a program needn't handle non-finite values. No bound on the sum of `free_mask` on one device may be relied on, other than what follows from the above.
Results may differ from a plain program's by a relative error of at most 0.0003.
Values sent between devices are 32-bit elements; how exact they have to be, the bound alone decides.
A program may use at most 64 MiB of HBM per device.

v0:
```python
import math
import jax
import jax.numpy as jnp
from jax import lax
from jax.sharding import PartitionSpec as P

ITERS = 2


def padded_2(shard, sides, width):
    for axis, dim in sides:
        count, length = (lax.axis_size(axis), shard.shape[dim])
        up = [(i, (i + 1) % count) for i in range(count - 1)]
        down = [(j, i) for i, j in up]
        last = lax.slice_in_dim(shard, length - width, length, axis=dim)
        leading = lax.slice_in_dim(shard, 0, width, axis=dim)
        before = lax.ppermute(last, axis, up)
        after = lax.ppermute(leading, axis, down)
        shard = jnp.concatenate([before, shard, after], axis=dim)
    return shard


def on_device(right_side, viscosity, free_mask, coarse_basis, gram_inverse):
    high = lax.Precision.HIGHEST
    components, patch_rows, patch_cols = right_side.shape
    columns = coarse_basis.shape[0]
    unknowns = (
        components * patch_rows * patch_cols * lax.axis_size("row") * lax.axis_size("col") * columns
    )
    coarse_scale = 1.0 / (32.0 * math.sqrt(float(unknowns)))
    viscosity_pad = padded_2(viscosity, (("row", 0), ("col", 1)), 1)
    face_north = 0.5 * (viscosity + viscosity_pad[2:, 1:-1])
    face_south = 0.5 * (viscosity + viscosity_pad[:-2, 1:-1])
    face_east = 0.5 * (viscosity + viscosity_pad[1:-1, 2:])
    face_west = 0.5 * (viscosity + viscosity_pad[1:-1, :-2])
    diagonal = 1.0 + face_north + face_south + face_east + face_west
    unfixed = free_mask.astype(jnp.float32)
    jacobi = unfixed / diagonal + (1.0 - unfixed)
    basis_rows = coarse_basis.reshape(columns, -1)

    def solve_coarse(coarse_dot):
        coeff_part = jnp.dot(gram_inverse, coarse_dot, precision=high) * coarse_scale
        return lax.all_gather(coeff_part, "col", axis=0, tiled=True)

    def precondition(residual, coarse_dot, weighted_sq):
        coeffs = solve_coarse(coarse_dot)
        smoothed = jacobi * residual + jnp.dot(coeffs, basis_rows, precision=high).reshape(
            residual.shape
        )
        return (smoothed, weighted_sq + jnp.dot(coarse_dot, coeffs, precision=high))

    solution = jnp.zeros_like(right_side)
    residual = right_side
    coarse_dot, weighted_sq = lax.psum(
        (
            jnp.dot(basis_rows, residual.reshape(-1), precision=high),
            jnp.sum(jacobi * residual * residual),
        ),
        ("row", "col"),
    )
    direction, energy = precondition(residual, coarse_dot, weighted_sq)
    for iteration in range(ITERS):
        masked = unfixed * direction
        padded = padded_2(masked, (("row", 1), ("col", 2)), 1)
        stencil = diagonal * masked - (
            face_north * padded[:, 2:, 1:-1]
            + face_south * padded[:, :-2, 1:-1]
            + face_east * padded[:, 1:-1, 2:]
            + face_west * padded[:, 1:-1, :-2]
        )
        applied = unfixed * stencil + (1.0 - unfixed) * direction
        if iteration + 1 < ITERS:
            curve_sum, image_coarse, cross_term, image_sq = lax.psum(
                (
                    jnp.sum(direction * applied),
                    jnp.dot(basis_rows, applied.reshape(-1), precision=high),
                    jnp.sum(jacobi * residual * applied),
                    jnp.sum(jacobi * applied * applied),
                ),
                ("row", "col"),
            )
            step_len = energy / curve_sum
            solution = step_len * direction
            residual = residual - step_len * applied
            coarse_dot = coarse_dot - step_len * image_coarse
            weighted_sq = weighted_sq - 2.0 * step_len * cross_term + step_len * step_len * image_sq
            smoothed, energy_new = precondition(residual, coarse_dot, weighted_sq)
            direction = smoothed + energy_new / energy * direction
            energy = energy_new
        else:
            curve_sum = lax.psum(jnp.sum(direction * applied), ("row", "col"))
            step_len = energy / curve_sum
            solution = solution + step_len * direction
            residual = residual - step_len * applied
    return (solution, residual)


def solution(mesh):
    in_specs = (
        P(None, "row", "col"),
        P("row", "col"),
        P(None, "row", "col"),
        P(None, None, "row", "col"),
        P("col", None),
    )
    out_specs = (P(None, "row", "col"), P(None, "row", "col"))
    return jax.shard_map(
        on_device, mesh=mesh, in_specs=in_specs, out_specs=out_specs, check_vma=False
    )
```

profile of v0, /device:TPU:0, one launch (start us, length us, event | category | flops | bytes accessed | tf_op | source)
XLA Modules:
  0.0 198.3 jit_solution(4688476039508117926)
XLA Ops:
  0.6 0.0 copy-start
  0.6 0.8 fusion.55
  1.4 1.3 collective-permute-start
  2.7 5.5 %collective-permute-start.1 = (f32[1,128]{1,0:T(1,128)S(1)}, f32[1,128]{1,0:T(1,128)S(1)}, u32[]{:S(2)}, u32[]{:S(2)}) collective-permute-start(f32[1,128]{1,0:T(1,128)S(1)} %get-tuple-element.33), channel_id=1, source_target_pairs={{0,4},{4,8},{8,12},{12,16},{16,20},{20,24},{24,28},{1,5},{5,9},{9,... | collective-permute-start | bytes 1544 | tf_op jit(solution)/shard_map/ppermute | solution.py:17
  8.2 1.3 copy.32
  9.5 0.0 copy-start.1
  9.5 0.0 copy-start.2
  9.5 0.1 copy.22
  9.7 1.0 copy-done.1
  10.7 0.0 copy-done.2
  10.7 0.7 convolution_bitcast_fusion.3
  11.4 41.9 %psum.50 = f32[64]{0:T(128)S(1)} all-reduce(f32[64]{0:T(128)S(1)} %convolution_bitcast_fusion.3), channel_id=1, replica_groups=mesh['row'=8,'col'=4] {'row','col'}, use_global_device_ids=true, to_apply=%region_2.0 | all-reduce | flops 64 | bytes 512 | tf_op jit(solution)/shard_map/psum | solution.py:54
  53.3 0.0 copy-done
  53.3 0.1 fusion.1
  53.4 0.0 copy-start.5
  53.4 0.7 copy-done.5
  54.1 0.6 dynamic-slice
  55.3 0.2 dynamic-update-slice
  55.5 5.8 %all-reduce = f32[64]{0:T(128)S(1)} all-reduce(f32[64]{0:T(128)S(1)} %dynamic-update-slice), channel_id=1, replica_groups=mesh['row'=8,'col'=4] {'col'}, use_global_device_ids=true, to_apply=%add | all-reduce | flops 64 | bytes 512
  61.3 0.0 copy-start.4
  61.3 0.6 fusion.4
  61.9 0.0 collective-permute-done
  61.9 0.0 collective-permute-done.1
  61.9 0.1 copy-done.4
  62.0 0.0 copy-start.3
  62.0 0.1 fusion.54
  62.1 1.3 collective-permute-start.2
  63.4 3.0 %collective-permute-start.3 = (f32[10,1]{1,0:T(8,128)S(1)}, f32[10,1]{1,0:T(8,128)S(1)}, u32[]{:S(2)}, u32[]{:S(2)}) collective-permute-start(f32[10,1]{1,0:T(8,128)S(1)} %get-tuple-element.31), channel_id=1, source_target_pairs={{0,1},{1,2},{2,3},{4,5},{5,6},{6,7},{8,9},{9,10},{10,11},{12,13},{... | collective-permute-start | bytes 128 | tf_op jit(solution)/shard_map/ppermute | solution.py:17
  66.4 0.0 collective-permute-done.2
  66.5 0.8 collective-permute-done.3
  67.3 0.1 add_add_fusion
  67.3 0.0 copy-done.3
  67.4 1.3 collective-permute-start.4
  68.7 4.8 %collective-permute-start.5 = (f32[3,1,128]{2,1,0:T(1,128)S(1)}, f32[3,1,128]{2,1,0:T(1,128)S(1)}, u32[]{:S(2)}, u32[]{:S(2)}) collective-permute-start(f32[3,1,128]{2,1,0:T(1,128)S(1)} %get-tuple-element.29), channel_id=1, source_target_pairs={{0,4},{4,8},{8,12},{12,16},{16,20},{20,24},{24,28},{1,5},{5,9},{9,... | collective-permute-start | bytes 4616 | tf_op jit(solution)/shard_map/ppermute | solution.py:17
  73.5 0.0 collective-permute-done.4
  73.5 1.3 collective-permute-done.5
  74.8 0.1 fusion.51
  74.9 2.3 %collective-permute-start.7 = (f32[3,10,1]{2,1,0:T(8,128)S(1)}, f32[3,10,1]{2,1,0:T(8,128)S(1)}, u32[]{:S(2)}, u32[]{:S(2)}) collective-permute-start(f32[3,10,1]{2,1,0:T(8,128)S(1)} %get-tuple-element.26), channel_id=1, source_target_pairs={{0,1},{1,2},{2,3},{4,5},{5,6},{6,7},{8,9},{9,10},{10,11},{12,13},{... | collective-permute-start | bytes 368 | tf_op jit(solution)/shard_map/ppermute | solution.py:17
  77.2 1.3 collective-permute-start.6
  78.5 0.7 multiply_reduce_fusion.5
  79.1 0.0 collective-permute-done.7
  79.1 4.0 %collective-permute-done.6 = f32[3,10,1]{2,1,0:T(8,128)S(1)} collective-permute-done((f32[3,10,1]{2,1,0:T(8,128)S(1)}, f32[3,10,1]{2,1,0:T(8,128)S(1)}, u32[]{:S(2)}, u32[]{:S(2)}) %collective-permute-start.6) | collective-permute-done | bytes 152 | tf_op jit(solution)/shard_map/ppermute | solution.py:18
  83.2 0.7 fusion.8
  83.9 0.7 convolution_bitcast_fusion.1
  84.6 42.6 %all-reduce.2 = (f32[64]{0:T(128)S(1)}, f32[]{:T(128)}, f32[]{:T(128)}, f32[]{:T(128)}, f32[]{:T(128)}) all-reduce(f32[64]{0:T(128)S(1)} %convolution_bitcast_fusion.1, f32[]{:T(128)} %get-tuple-element.4, f32[]{:T(128)} %get-tuple-element.5, f32[]{:T(128)} %get-tuple-element.3, ...), channel_id=1, replica_groups=mesh['row'=8,'col'=4] {'row','col'}, use_global_device_ids=true, to_apply=%region_9.0 | all-reduce | flops 68 | bytes 544 | tf_op jit(solution)/shard_map/psum | solution.py:73
  129.1 0.1 fusion
  129.2 0.2 dynamic-update-slice.1
  129.5 7.6 %all-reduce.1 = f32[64]{0:T(128)S(1)} all-reduce(f32[64]{0:T(128)S(1)} %dynamic-update-slice.1), channel_id=1, replica_groups=mesh['row'=8,'col'=4] {'col'}, use_global_device_ids=true, to_apply=%add.1 | all-reduce | flops 64 | bytes 512
  137.1 0.6 multiply_reduce_fusion.4
  137.7 0.6 fusion.2
  140.8 1.3 collective-permute-start.8
  142.1 4.5 %collective-permute-start.9 = (f32[3,1,128]{2,1,0:T(1,128)S(1)}, f32[3,1,128]{2,1,0:T(1,128)S(1)}, u32[]{:S(2)}, u32[]{:S(2)}) collective-permute-start(f32[3,1,128]{2,1,0:T(1,128)S(1)} %get-tuple-element.27), channel_id=1, source_target_pairs={{0,4},{4,8},{8,12},{12,16},{16,20},{20,24},{24,28},{1,5},{5,9},{9,... | collective-permute-start | bytes 4616 | tf_op jit(solution)/shard_map/ppermute | solution.py:17
  146.7 0.0 collective-permute-done.8
  146.7 1.3 collective-permute-done.9
  148.0 0.1 fusion.50
  148.0 1.3 collective-permute-start.11
  149.3 1.3 collective-permute-start.10
  150.6 0.0 collective-permute-done.11
  150.6 2.6 %collective-permute-done.10 = f32[3,10,1]{2,1,0:T(8,128)S(1)} collective-permute-done((f32[3,10,1]{2,1,0:T(8,128)S(1)}, f32[3,10,1]{2,1,0:T(8,128)S(1)}, u32[]{:S(2)}, u32[]{:S(2)}) %collective-permute-start.10) | collective-permute-done | bytes 152 | tf_op jit(solution)/shard_map/ppermute | solution.py:18
  153.3 0.7 multiply_reduce_fusion
  154.0 43.0 %psum.55 = f32[]{:T(128)} all-reduce(f32[]{:T(128)} %get-tuple-element.11), channel_id=1, replica_groups=mesh['row'=8,'col'=4] {'row','col'}, use_global_device_ids=true, to_apply=%region_11.0 | all-reduce | flops 1 | bytes 8 | tf_op jit(solution)/shard_map/psum | solution.py:91
  197.7 0.6 multiply_subtract_fusion
  (9 shorter events, 0.1 us)
Async XLA Ops:
  0.6 52.6 %copy-start = (f32[16,64]{1,0:T(8,128)S(1)}, f32[16,64]{1,0:T(8,128)}, u32[]{:S(2)}) copy-start(f32[16,64]{1,0:T(8,128)} %param.9) | copy-start | bytes 12292
  1.4 60.5 %collective-permute-start = (f32[1,128]{1,0:T(1,128)S(1)}, f32[1,128]{1,0:T(1,128)S(1)}, u32[]{:S(2)}, u32[]{:S(2)}) collective-permute-start(f32[1,128]{1,0:T(1,128)S(1)} %get-tuple-element.34), channel_id=1, source_target_pairs={{4,0},{8,4},{12,8},{16,12},{20,16},{24,20},{28,24},{5,1},{9,5},{13... | collective-permute-start | bytes 1544 | tf_op jit(solution)/shard_map/ppermute | solution.py:18
  2.7 59.2 %collective-permute-start.1 = (f32[1,128]{1,0:T(1,128)S(1)}, f32[1,128]{1,0:T(1,128)S(1)}, u32[]{:S(2)}, u32[]{:S(2)}) collective-permute-start(f32[1,128]{1,0:T(1,128)S(1)} %get-tuple-element.33), channel_id=1, source_target_pairs={{0,4},{4,8},{8,12},{12,16},{16,20},{20,24},{24,28},{1,5},{5,9},{9,... | collective-permute-start | bytes 1544 | tf_op jit(solution)/shard_map/ppermute | solution.py:17
  9.5 1.1 copy-start.1
  9.5 1.1 copy-start.2
  53.4 0.7 copy-start.5
  61.3 0.7 copy-start.4
  62.0 5.3 %copy-start.3 = (s32[3,8,128]{2,1,0:T(8,128)S(1)}, s32[3,8,128]{2,1,0:T(8,128)}, u32[]{:S(2)}) copy-start(s32[3,8,128]{2,1,0:T(8,128)} %param.7) | copy-start | bytes 36868
  62.1 4.3 %collective-permute-start.2 = (f32[10,1]{1,0:T(8,128)S(1)}, f32[10,1]{1,0:T(8,128)S(1)}, u32[]{:S(2)}, u32[]{:S(2)}) collective-permute-start(f32[10,1]{1,0:T(8,128)S(1)} %get-tuple-element.32), channel_id=1, source_target_pairs={{1,0},{2,1},{3,2},{5,4},{6,5},{7,6},{9,8},{10,9},{11,10},{13,12},{... | collective-permute-start | bytes 128 | tf_op jit(solution)/shard_map/ppermute | solution.py:18
  63.4 3.8 %collective-permute-start.3 = (f32[10,1]{1,0:T(8,128)S(1)}, f32[10,1]{1,0:T(8,128)S(1)}, u32[]{:S(2)}, u32[]{:S(2)}) collective-permute-start(f32[10,1]{1,0:T(8,128)S(1)} %get-tuple-element.31), channel_id=1, source_target_pairs={{0,1},{1,2},{2,3},{4,5},{5,6},{6,7},{8,9},{9,10},{10,11},{12,13},{... | collective-permute-start | bytes 128 | tf_op jit(solution)/shard_map/ppermute | solution.py:17
  67.4 6.1 %collective-permute-start.4 = (f32[3,1,128]{2,1,0:T(1,128)S(1)}, f32[3,1,128]{2,1,0:T(1,128)S(1)}, u32[]{:S(2)}, u32[]{:S(2)}) collective-permute-start(f32[3,1,128]{2,1,0:T(1,128)S(1)} %get-tuple-element.30), channel_id=1, source_target_pairs={{4,0},{8,4},{12,8},{16,12},{20,16},{24,20},{28,24},{5,1},{9,5},{13... | collective-permute-start | bytes 4616 | tf_op jit(solution)/shard_map/ppermute | solution.py:18
  68.7 6.1 %collective-permute-start.5 = (f32[3,1,128]{2,1,0:T(1,128)S(1)}, f32[3,1,128]{2,1,0:T(1,128)S(1)}, u32[]{:S(2)}, u32[]{:S(2)}) collective-permute-start(f32[3,1,128]{2,1,0:T(1,128)S(1)} %get-tuple-element.29), channel_id=1, source_target_pairs={{0,4},{4,8},{8,12},{12,16},{16,20},{20,24},{24,28},{1,5},{5,9},{9,... | collective-permute-start | bytes 4616 | tf_op jit(solution)/shard_map/ppermute | solution.py:17
  74.9 4.3 %collective-permute-start.7 = (f32[3,10,1]{2,1,0:T(8,128)S(1)}, f32[3,10,1]{2,1,0:T(8,128)S(1)}, u32[]{:S(2)}, u32[]{:S(2)}) collective-permute-start(f32[3,10,1]{2,1,0:T(8,128)S(1)} %get-tuple-element.26), channel_id=1, source_target_pairs={{0,1},{1,2},{2,3},{4,5},{5,6},{6,7},{8,9},{9,10},{10,11},{12,13},{... | collective-permute-start | bytes 368 | tf_op jit(solution)/shard_map/ppermute | solution.py:17
  77.2 6.0 %collective-permute-start.6 = (f32[3,10,1]{2,1,0:T(8,128)S(1)}, f32[3,10,1]{2,1,0:T(8,128)S(1)}, u32[]{:S(2)}, u32[]{:S(2)}) collective-permute-start(f32[3,10,1]{2,1,0:T(8,128)S(1)} %get-tuple-element.25), channel_id=1, source_target_pairs={{1,0},{2,1},{3,2},{5,4},{6,5},{7,6},{9,8},{10,9},{11,10},{13,12},{... | collective-permute-start | bytes 368 | tf_op jit(solution)/shard_map/ppermute | solution.py:18
  140.8 5.9 %collective-permute-start.8 = (f32[3,1,128]{2,1,0:T(1,128)S(1)}, f32[3,1,128]{2,1,0:T(1,128)S(1)}, u32[]{:S(2)}, u32[]{:S(2)}) collective-permute-start(f32[3,1,128]{2,1,0:T(1,128)S(1)} %get-tuple-element.28), channel_id=1, source_target_pairs={{4,0},{8,4},{12,8},{16,12},{20,16},{24,20},{28,24},{5,1},{9,5},{13... | collective-permute-start | bytes 4616 | tf_op jit(solution)/shard_map/ppermute | solution.py:18
  142.1 5.8 %collective-permute-start.9 = (f32[3,1,128]{2,1,0:T(1,128)S(1)}, f32[3,1,128]{2,1,0:T(1,128)S(1)}, u32[]{:S(2)}, u32[]{:S(2)}) collective-permute-start(f32[3,1,128]{2,1,0:T(1,128)S(1)} %get-tuple-element.27), channel_id=1, source_target_pairs={{0,4},{4,8},{8,12},{12,16},{16,20},{20,24},{24,28},{1,5},{5,9},{9,... | collective-permute-start | bytes 4616 | tf_op jit(solution)/shard_map/ppermute | solution.py:17
  148.0 2.6 %collective-permute-start.11 = (f32[3,10,1]{2,1,0:T(8,128)S(1)}, f32[3,10,1]{2,1,0:T(8,128)S(1)}, u32[]{:S(2)}, u32[]{:S(2)}) collective-permute-start(f32[3,10,1]{2,1,0:T(8,128)S(1)} %get-tuple-element.24), channel_id=1, source_target_pairs={{0,1},{1,2},{2,3},{4,5},{5,6},{6,7},{8,9},{9,10},{10,11},{12,13},{... | collective-permute-start | bytes 368 | tf_op jit(solution)/shard_map/ppermute | solution.py:17
  149.3 3.9 %collective-permute-start.10 = (f32[3,10,1]{2,1,0:T(8,128)S(1)}, f32[3,10,1]{2,1,0:T(8,128)S(1)}, u32[]{:S(2)}, u32[]{:S(2)}) collective-permute-start(f32[3,10,1]{2,1,0:T(8,128)S(1)} %get-tuple-element.23), channel_id=1, source_target_pairs={{1,0},{2,1},{3,2},{5,4},{6,5},{7,6},{9,8},{10,9},{11,10},{13,12},{... | collective-permute-start | bytes 368 | tf_op jit(solution)/shard_map/ppermute | solution.py:18
where the time goes:
time: 199 us; the launch traced here: 198 us
  blocking collectives  141 us (71%)
  starting transfers between devices  29.2 us (15%)
  waiting for transfers between devices  10 us (5%)
  between operations  6.67 us (3%)
  local copies, waits for them, and re-layouts  5.22 us (3%)
  other arithmetic  3.45 us (2%)
  matrix products  2.83 us (1%)
    psum x1, blocking collectives, on_device(): curve_sum = lax.psum(jnp.sum(direction * applied), ('row', 'col'))  43 us
    psum x1, blocking collectives, on_device(): lax.psum((jnp.sum(direction * applied), jnp.dot(basis_rows, applied.resha...  42.6 us
    psum x1, blocking collectives, on_device(): lax.psum((jnp.dot(basis_rows, residual.reshape(-1), precision=high), jnp....  41.9 us
    ppermute x6, starting transfers between devices, padded_2(): before = lax.ppermute(last, axis, up)  21.5 us
    unnamed x2, blocking collectives  13.4 us
    ppermute x6, starting transfers between devices, padded_2(): after = lax.ppermute(leading, axis, down)  7.73 us
    ppermute x6, waiting for transfers between devices, padded_2(): after = lax.ppermute(leading, axis, down)  6.67 us
    unnamed x19, local copies, waits for them, and re-layouts  4.22 us
  transfers between devices with their start and end apart: 12, of which 5 were waited for; matrix products, arithmetic and copies ran while one was open for 2% of the time, Pallas kernels for 0%

commit v1 on v0

--- a/solution.py
+++ b/solution.py
@@ -52,11 +52,14 @@
     solution = jnp.zeros_like(right_side)
     residual = right_side
     coarse_dot, weighted_sq = lax.psum(
-        (
-            jnp.dot(basis_rows, residual.reshape(-1), precision=high),
-            jnp.sum(jacobi * residual * residual),
+        lax.psum(
+            (
+                jnp.dot(basis_rows, residual.reshape(-1), precision=high),
+                jnp.sum(jacobi * residual * residual),
+            ),
+            "col",
         ),
-        ("row", "col"),
+        "row",
     )
     direction, energy = precondition(residual, coarse_dot, weighted_sq)
     for iteration in range(ITERS):

time: 199 us -> 208 us (1.045)
  blocking collectives: 141 us -> 149 us
    psum x0 -> x2, blocking collectives: none -> 39.8 us  [on_device(): lax.psum(lax.psum((jnp.dot(basis_rows, residual.reshape(-1), precision=hi...]
    psum x1 -> x2, blocking collectives: 41.9 us -> 15.3 us  [on_device(): lax.psum((jnp.dot(basis_rows, residual.reshape(-1), precision=high), jnp....]
    psum x1, blocking collectives: 42.6 us -> 37.3 us  [on_device(): lax.psum((jnp.sum(direction * applied), jnp.dot(basis_rows, applied.resha...]
where the time goes in v1:
time: 208 us; the launch traced here: 207 us
  blocking collectives  149 us (72%)
  starting transfers between devices  28.5 us (14%)
  waiting for transfers between devices  11.2 us (5%)
  between operations  6.74 us (3%)
  local copies, waits for them, and re-layouts  5.22 us (3%)
  other arithmetic  3.45 us (2%)
  matrix products  2.83 us (1%)
    psum x1, blocking collectives, on_device(): curve_sum = lax.psum(jnp.sum(direction * applied), ('row', 'col'))  44.3 us
    psum x2, blocking collectives, on_device(): lax.psum(lax.psum((jnp.dot(basis_rows, residual.reshape(-1), precision=hi...  39.8 us
    psum x1, blocking collectives, on_device(): lax.psum((jnp.sum(direction * applied), jnp.dot(basis_rows, applied.resha...  37.3 us
    ppermute x6, starting transfers between devices, padded_2(): before = lax.ppermute(last, axis, up)  20.8 us
    psum x2, blocking collectives, on_device(): lax.psum((jnp.dot(basis_rows, residual.reshape(-1), precision=high), jnp....  15.3 us
    unnamed x2, blocking collectives  12.5 us
    ppermute x6, waiting for transfers between devices, padded_2(): after = lax.ppermute(leading, axis, down)  7.88 us
    ppermute x6, starting transfers between devices, padded_2(): after = lax.ppermute(leading, axis, down)  7.73 us
  transfers between devices with their start and end apart: 12, of which 5 were waited for; matrix products, arithmetic and copies ran while one was open for 2% of the time, Pallas kernels for 0%

profile of v1, /device:TPU:0, one launch (start us, length us, event | category | flops | bytes accessed | tf_op | source)
XLA Modules:
  0.0 207.2 jit_solution(10395584745322814752)
XLA Ops:
  0.6 0.0 copy-start
  0.6 0.8 fusion.55
  1.4 1.3 collective-permute-start
  2.7 5.5 %collective-permute-start.1 = (f32[1,128]{1,0:T(1,128)S(1)}, f32[1,128]{1,0:T(1,128)S(1)}, u32[]{:S(2)}, u32[]{:S(2)}) collective-permute-start(f32[1,128]{1,0:T(1,128)S(1)} %get-tuple-element.32), channel_id=1, source_target_pairs={{0,4},{4,8},{8,12},{12,16},{16,20},{20,24},{24,28},{1,5},{5,9},{9,... | collective-permute-start | bytes 1544 | tf_op jit(solution)/shard_map/ppermute | solution.py:17
  8.2 1.3 copy.32
  9.5 0.0 copy-start.1
  9.5 0.0 copy-start.2
  9.5 0.1 copy.22
  9.7 1.0 copy-done.1
  10.7 0.0 copy-done.2
  10.7 0.7 convolution_bitcast_fusion.3
  11.4 6.5 %psum.65 = f32[64]{0:T(128)S(1)} all-reduce(f32[64]{0:T(128)S(1)} %convolution_bitcast_fusion.3), channel_id=1, replica_groups=mesh['row'=8,'col'=4] {'col'}, use_global_device_ids=true, to_apply=%region_3.0 | all-reduce | flops 64 | bytes 512 | tf_op jit(solution)/shard_map/psum | solution.py:55
  17.9 19.8 %psum.66 = f32[64]{0:T(128)S(1)} all-reduce(f32[64]{0:T(128)S(1)} %psum.65), channel_id=1, replica_groups=mesh['row'=8,'col'=4] {'row'}, use_global_device_ids=true, to_apply=%region_4.0 | all-reduce | flops 64 | bytes 512 | tf_op jit(solution)/shard_map/psum | solution.py:54
  37.7 0.0 copy-done
  37.7 0.1 fusion.1
  37.8 0.7 copy-done.5
  38.5 0.6 dynamic-slice
  39.7 0.2 dynamic-update-slice
  40.0 5.6 %all-reduce = f32[64]{0:T(128)S(1)} all-reduce(f32[64]{0:T(128)S(1)} %dynamic-update-slice), channel_id=1, replica_groups=mesh['row'=8,'col'=4] {'col'}, use_global_device_ids=true, to_apply=%add | all-reduce | flops 64 | bytes 512
  45.6 0.0 copy-start.4
  45.6 0.6 fusion.4
  46.2 0.0 collective-permute-done
  46.2 0.0 collective-permute-done.1
  46.2 0.1 copy-done.4
  46.3 0.0 copy-start.3
  46.3 0.1 fusion.54
  46.4 1.3 collective-permute-start.2
  47.7 3.0 %collective-permute-start.3 = (f32[10,1]{1,0:T(8,128)S(1)}, f32[10,1]{1,0:T(8,128)S(1)}, u32[]{:S(2)}, u32[]{:S(2)}) collective-permute-start(f32[10,1]{1,0:T(8,128)S(1)} %get-tuple-element.30), channel_id=1, source_target_pairs={{0,1},{1,2},{2,3},{4,5},{5,6},{6,7},{8,9},{9,10},{10,11},{12,13},{... | collective-permute-start | bytes 128 | tf_op jit(solution)/shard_map/ppermute | solution.py:17
  50.7 0.0 collective-permute-done.2
  50.7 0.8 collective-permute-done.3
  51.5 0.1 add_add_fusion
  51.6 0.0 copy-done.3
  51.6 1.3 collective-permute-start.4
  52.9 4.5 %collective-permute-start.5 = (f32[3,1,128]{2,1,0:T(1,128)S(1)}, f32[3,1,128]{2,1,0:T(1,128)S(1)}, u32[]{:S(2)}, u32[]{:S(2)}) collective-permute-start(f32[3,1,128]{2,1,0:T(1,128)S(1)} %get-tuple-element.28), channel_id=1, source_target_pairs={{0,4},{4,8},{8,12},{12,16},{16,20},{20,24},{24,28},{1,5},{5,9},{9,... | collective-permute-start | bytes 4616 | tf_op jit(solution)/shard_map/ppermute | solution.py:17
  57.5 0.0 collective-permute-done.4
  57.5 1.3 collective-permute-done.5
  58.8 0.1 fusion.51
  58.9 1.8 collective-permute-start.7
  60.7 1.3 collective-permute-start.6
  62.0 0.0 collective-permute-done.7
  62.0 4.7 %collective-permute-done.6 = f32[3,10,1]{2,1,0:T(8,128)S(1)} collective-permute-done((f32[3,10,1]{2,1,0:T(8,128)S(1)}, f32[3,10,1]{2,1,0:T(8,128)S(1)}, u32[]{:S(2)}, u32[]{:S(2)}) %collective-permute-start.6) | collective-permute-done | bytes 152 | tf_op jit(solution)/shard_map/ppermute | solution.py:18
  66.7 0.8 fusion.8
  67.5 8.8 %psum.63 = f32[]{:T(128)} all-reduce(f32[]{:T(128)} %get-tuple-element.4), channel_id=1, replica_groups=mesh['row'=8,'col'=4] {'col'}, use_global_device_ids=true, to_apply=%region_1.0 | all-reduce | flops 1 | bytes 8 | tf_op jit(solution)/shard_map/psum | solution.py:55
  76.3 0.6 multiply_reduce_fusion.5
  77.0 20.0 %psum.64 = f32[]{:T(128)} all-reduce(f32[]{:T(128)} %psum.63), channel_id=1, replica_groups=mesh['row'=8,'col'=4] {'row'}, use_global_device_ids=true, to_apply=%region_2.0 | all-reduce | flops 1 | bytes 8 | tf_op jit(solution)/shard_map/psum | solution.py:54
  97.0 0.7 convolution_bitcast_fusion.1
  99.0 37.3 %all-reduce.2 = (f32[64]{0:T(128)S(1)}, f32[]{:T(128)}, f32[]{:T(128)}, f32[]{:T(128)}) all-reduce(f32[64]{0:T(128)S(1)} %convolution_bitcast_fusion.1, f32[]{:T(128)} %get-tuple-element.5, f32[]{:T(128)} %get-tuple-element.3, f32[]{:T(128)} %get-tuple-element.2), channel_id=1, replica_groups=mesh['row'=8,'col'=4] {'row','col'}, use_global_device_ids=true, to_apply=%region_11.0 | all-reduce | flops 67 | bytes 536 | tf_op jit(solution)/shard_map/psum | solution.py:76
  136.9 0.1 fusion
  137.1 0.2 dynamic-update-slice.1
  137.3 6.9 %all-reduce.1 = f32[64]{0:T(128)S(1)} all-reduce(f32[64]{0:T(128)S(1)} %dynamic-update-slice.1), channel_id=1, replica_groups=mesh['row'=8,'col'=4] {'col'}, use_global_device_ids=true, to_apply=%add.1 | all-reduce | flops 64 | bytes 512
  144.2 0.6 multiply_reduce_fusion.4
  144.8 0.6 fusion.2
  147.9 1.3 collective-permute-start.8
  149.2 4.5 %collective-permute-start.9 = (f32[3,1,128]{2,1,0:T(1,128)S(1)}, f32[3,1,128]{2,1,0:T(1,128)S(1)}, u32[]{:S(2)}, u32[]{:S(2)}) collective-permute-start(f32[3,1,128]{2,1,0:T(1,128)S(1)} %get-tuple-element.26), channel_id=1, source_target_pairs={{0,4},{4,8},{8,12},{12,16},{16,20},{20,24},{24,28},{1,5},{5,9},{9,... | collective-permute-start | bytes 4616 | tf_op jit(solution)/shard_map/ppermute | solution.py:17
  153.8 0.0 collective-permute-done.8
  153.8 1.3 collective-permute-done.9
  155.1 0.1 fusion.50
  155.2 1.3 collective-permute-start.11
  156.5 1.3 collective-permute-start.10
  157.8 0.0 collective-permute-done.11
  157.8 3.2 %collective-permute-done.10 = f32[3,10,1]{2,1,0:T(8,128)S(1)} collective-permute-done((f32[3,10,1]{2,1,0:T(8,128)S(1)}, f32[3,10,1]{2,1,0:T(8,128)S(1)}, u32[]{:S(2)}, u32[]{:S(2)}) %collective-permute-start.10) | collective-permute-done | bytes 152 | tf_op jit(solution)/shard_map/ppermute | solution.py:18
  160.9 0.7 multiply_reduce_fusion
  161.6 44.3 %psum.71 = f32[]{:T(128)} all-reduce(f32[]{:T(128)} %get-tuple-element.10), channel_id=1, replica_groups=mesh['row'=8,'col'=4] {'row','col'}, use_global_device_ids=true, to_apply=%region_13.0 | all-reduce | flops 1 | bytes 8 | tf_op jit(solution)/shard_map/psum | solution.py:94
  206.6 0.6 multiply_subtract_fusion
  (10 shorter events, 0.1 us)
Async XLA Ops:
  0.6 37.1 %copy-start = (f32[16,64]{1,0:T(8,128)S(1)}, f32[16,64]{1,0:T(8,128)}, u32[]{:S(2)}) copy-start(f32[16,64]{1,0:T(8,128)} %param.9) | copy-start | bytes 12292
  1.4 44.8 %collective-permute-start = (f32[1,128]{1,0:T(1,128)S(1)}, f32[1,128]{1,0:T(1,128)S(1)}, u32[]{:S(2)}, u32[]{:S(2)}) collective-permute-start(f32[1,128]{1,0:T(1,128)S(1)} %get-tuple-element.33), channel_id=1, source_target_pairs={{4,0},{8,4},{12,8},{16,12},{20,16},{24,20},{28,24},{5,1},{9,5},{13... | collective-permute-start | bytes 1544 | tf_op jit(solution)/shard_map/ppermute | solution.py:18
  2.7 43.5 %collective-permute-start.1 = (f32[1,128]{1,0:T(1,128)S(1)}, f32[1,128]{1,0:T(1,128)S(1)}, u32[]{:S(2)}, u32[]{:S(2)}) collective-permute-start(f32[1,128]{1,0:T(1,128)S(1)} %get-tuple-element.32), channel_id=1, source_target_pairs={{0,4},{4,8},{8,12},{12,16},{16,20},{20,24},{24,28},{1,5},{5,9},{9,... | collective-permute-start | bytes 1544 | tf_op jit(solution)/shard_map/ppermute | solution.py:17
  9.5 1.1 copy-start.1
  9.5 1.1 copy-start.2
  37.8 0.7 copy-start.5
  45.6 0.7 copy-start.4
  46.3 5.3 %copy-start.3 = (s32[3,8,128]{2,1,0:T(8,128)S(1)}, s32[3,8,128]{2,1,0:T(8,128)}, u32[]{:S(2)}) copy-start(s32[3,8,128]{2,1,0:T(8,128)} %param.7) | copy-start | bytes 36868
  46.4 4.3 %collective-permute-start.2 = (f32[10,1]{1,0:T(8,128)S(1)}, f32[10,1]{1,0:T(8,128)S(1)}, u32[]{:S(2)}, u32[]{:S(2)}) collective-permute-start(f32[10,1]{1,0:T(8,128)S(1)} %get-tuple-element.31), channel_id=1, source_target_pairs={{1,0},{2,1},{3,2},{5,4},{6,5},{7,6},{9,8},{10,9},{11,10},{13,12},{... | collective-permute-start | bytes 128 | tf_op jit(solution)/shard_map/ppermute | solution.py:18
  47.7 3.8 %collective-permute-start.3 = (f32[10,1]{1,0:T(8,128)S(1)}, f32[10,1]{1,0:T(8,128)S(1)}, u32[]{:S(2)}, u32[]{:S(2)}) collective-permute-start(f32[10,1]{1,0:T(8,128)S(1)} %get-tuple-element.30), channel_id=1, source_target_pairs={{0,1},{1,2},{2,3},{4,5},{5,6},{6,7},{8,9},{9,10},{10,11},{12,13},{... | collective-permute-start | bytes 128 | tf_op jit(solution)/shard_map/ppermute | solution.py:17
  51.6 5.9 %collective-permute-start.4 = (f32[3,1,128]{2,1,0:T(1,128)S(1)}, f32[3,1,128]{2,1,0:T(1,128)S(1)}, u32[]{:S(2)}, u32[]{:S(2)}) collective-permute-start(f32[3,1,128]{2,1,0:T(1,128)S(1)} %get-tuple-element.29), channel_id=1, source_target_pairs={{4,0},{8,4},{12,8},{16,12},{20,16},{24,20},{28,24},{5,1},{9,5},{13... | collective-permute-start | bytes 4616 | tf_op jit(solution)/shard_map/ppermute | solution.py:18
  52.9 5.8 %collective-permute-start.5 = (f32[3,1,128]{2,1,0:T(1,128)S(1)}, f32[3,1,128]{2,1,0:T(1,128)S(1)}, u32[]{:S(2)}, u32[]{:S(2)}) collective-permute-start(f32[3,1,128]{2,1,0:T(1,128)S(1)} %get-tuple-element.28), channel_id=1, source_target_pairs={{0,4},{4,8},{8,12},{12,16},{16,20},{20,24},{24,28},{1,5},{5,9},{9,... | collective-permute-start | bytes 4616 | tf_op jit(solution)/shard_map/ppermute | solution.py:17
  58.9 3.1 %collective-permute-start.7 = (f32[3,10,1]{2,1,0:T(8,128)S(1)}, f32[3,10,1]{2,1,0:T(8,128)S(1)}, u32[]{:S(2)}, u32[]{:S(2)}) collective-permute-start(f32[3,10,1]{2,1,0:T(8,128)S(1)} %get-tuple-element.25), channel_id=1, source_target_pairs={{0,1},{1,2},{2,3},{4,5},{5,6},{6,7},{8,9},{9,10},{10,11},{12,13},{... | collective-permute-start | bytes 368 | tf_op jit(solution)/shard_map/ppermute | solution.py:17
  60.7 6.0 %collective-permute-start.6 = (f32[3,10,1]{2,1,0:T(8,128)S(1)}, f32[3,10,1]{2,1,0:T(8,128)S(1)}, u32[]{:S(2)}, u32[]{:S(2)}) collective-permute-start(f32[3,10,1]{2,1,0:T(8,128)S(1)} %get-tuple-element.24), channel_id=1, source_target_pairs={{1,0},{2,1},{3,2},{5,4},{6,5},{7,6},{9,8},{10,9},{11,10},{13,12},{... | collective-permute-start | bytes 368 | tf_op jit(solution)/shard_map/ppermute | solution.py:18
  147.9 5.9 %collective-permute-start.8 = (f32[3,1,128]{2,1,0:T(1,128)S(1)}, f32[3,1,128]{2,1,0:T(1,128)S(1)}, u32[]{:S(2)}, u32[]{:S(2)}) collective-permute-start(f32[3,1,128]{2,1,0:T(1,128)S(1)} %get-tuple-element.27), channel_id=1, source_target_pairs={{4,0},{8,4},{12,8},{16,12},{20,16},{24,20},{28,24},{5,1},{9,5},{13... | collective-permute-start | bytes 4616 | tf_op jit(solution)/shard_map/ppermute | solution.py:18
  149.2 5.8 %collective-permute-start.9 = (f32[3,1,128]{2,1,0:T(1,128)S(1)}, f32[3,1,128]{2,1,0:T(1,128)S(1)}, u32[]{:S(2)}, u32[]{:S(2)}) collective-permute-start(f32[3,1,128]{2,1,0:T(1,128)S(1)} %get-tuple-element.26), channel_id=1, source_target_pairs={{0,4},{4,8},{8,12},{12,16},{16,20},{20,24},{24,28},{1,5},{5,9},{9,... | collective-permute-start | bytes 4616 | tf_op jit(solution)/shard_map/ppermute | solution.py:17
  155.2 2.6 %collective-permute-start.11 = (f32[3,10,1]{2,1,0:T(8,128)S(1)}, f32[3,10,1]{2,1,0:T(8,128)S(1)}, u32[]{:S(2)}, u32[]{:S(2)}) collective-permute-start(f32[3,10,1]{2,1,0:T(8,128)S(1)} %get-tuple-element.23), channel_id=1, source_target_pairs={{0,1},{1,2},{2,3},{4,5},{5,6},{6,7},{8,9},{9,10},{10,11},{12,13},{... | collective-permute-start | bytes 368 | tf_op jit(solution)/shard_map/ppermute | solution.py:17
  156.5 4.5 %collective-permute-start.10 = (f32[3,10,1]{2,1,0:T(8,128)S(1)}, f32[3,10,1]{2,1,0:T(8,128)S(1)}, u32[]{:S(2)}, u32[]{:S(2)}) collective-permute-start(f32[3,10,1]{2,1,0:T(8,128)S(1)} %get-tuple-element.22), channel_id=1, source_target_pairs={{1,0},{2,1},{3,2},{5,4},{6,5},{7,6},{9,8},{10,9},{11,10},{13,12},{... | collective-permute-start | bytes 368 | tf_op jit(solution)/shard_map/ppermute | solution.py:18
